TPU v7x, 32 devices: a whole 2x2x4 slice. The times are simulated.
32 devices in a mesh: grp: 2 (over x), blk: 16 (over z, y, core).
Axes of the slice: x: 2, y: 2, z: 4, core: 2. Of those that a mesh axis runs over, the one named last changes fastest.
Arguments:
- atoms: bfloat16 [16384, 512], P(('grp', 'blk')), parts along dimension 0, may hold values from -8 to 8
- edge_mask: int32 [32, 5, 512, 512], P(('grp', 'blk')), parts along dimension 0, may hold values from 0 to 1
- norm_gain: float32 [512], replicated, may hold values from 0.25 to 1.75
- w_query: bfloat16 [512, 512], replicated, may hold values from -3 to 3
- w_key: bfloat16 [512, 512], replicated, may hold values from -3 to 3
- w_value: bfloat16 [512, 512], replicated, may hold values from -0.25 to 0.25
- w_out: bfloat16 [512, 512], replicated, may hold values from -0.25 to 0.25
- bn_gain: float32 [512], replicated, may hold values from 0.25 to 1.75
- bn_shift: float32 [512], replicated, may hold values from -3 to 3
- w_up: bfloat16 [512, 1024], replicated, may hold values from -0.25 to 0.25
- w_down: bfloat16 [1024, 512], replicated, may hold values from -0.1875 to 0.1875
Outputs:
- updated: bfloat16 [16384, 512], P(('grp', 'blk')), parts along dimension 0
There are 2 independent parts, one for each index of `grp`. A program takes and returns all parts, laid end to end along the dimension named above; an argument that names none is the same for every part. Nothing has to cross between parts.
All inputs are finite; a program needn't handle non-finite values.
Results may differ from a plain program's by a relative error of at most 0.01.
The roundings to bfloat16 on the way count: a program that leaves them out, or rounds other values in their place, can miss the bound.
Values may be sent and summed in bfloat16 or wider, within the bound.
A program may use at most 128 MiB of HBM per device.

v0:
```python
import jax
import jax.numpy as jnp
from jax import lax
from jax.sharding import PartitionSpec as P

D = 512
HEADS = 8
HEAD_DIM = 64
REACH = 2


def passed_along(value, axis, steps):
    count = lax.axis_size(axis)
    pairs = [(source, (source + steps) % count) for source in range(count)]
    return lax.ppermute(value, axis, pairs)


def attend_block(state, query_heads, kv_block, allowed):
    running_top, running_total, running_sum = state
    tile_rows = query_heads.shape[0]
    key_heads = kv_block[0].reshape(tile_rows, HEADS, HEAD_DIM)
    value_heads = kv_block[1].reshape(tile_rows, HEADS, HEAD_DIM)
    score = jnp.einsum(
        "qhd,khd->hqk", query_heads, key_heads, preferred_element_type=jnp.float32
    ) * HEAD_DIM ** (-0.5)
    score = jnp.where(allowed[None], score, -1e30)
    new_top = jnp.maximum(running_top, jnp.max(score, axis=-1))
    factor = jnp.exp(running_top - new_top)
    expo = jnp.exp(score - new_top[:, :, None])
    new_total = running_total * factor + jnp.sum(expo, axis=-1)
    product = jnp.einsum(
        "hqk,khd->qhd", expo.astype(jnp.bfloat16), value_heads, preferred_element_type=jnp.float32
    )
    new_sum = running_sum * jnp.transpose(factor)[:, :, None] + product
    return (new_top, new_total, new_sum)


def project_pair(features, w_key, w_value):
    keys = jnp.dot(features, w_key, preferred_element_type=jnp.float32).astype(jnp.bfloat16)
    values = jnp.dot(features, w_value, preferred_element_type=jnp.float32).astype(jnp.bfloat16)
    return jnp.stack([keys, values])


def body(
    atoms, edge_mask, norm_gain, w_query, w_key, w_value, w_out, bn_gain, bn_shift, w_up, w_down
):
    tile_rows = atoms.shape[0]
    xfull = atoms.astype(jnp.float32)
    normed = (
        xfull * lax.rsqrt(jnp.mean(xfull * xfull, axis=-1, keepdims=True) + 1e-06) * norm_gain
    ).astype(jnp.bfloat16)
    query = jnp.dot(normed, w_query, preferred_element_type=jnp.float32).astype(jnp.bfloat16)
    kv_own = project_pair(normed, w_key, w_value)
    query_heads = query.reshape(tile_rows, HEADS, HEAD_DIM)
    masks = edge_mask[0]
    diagonal = lax.broadcasted_iota(jnp.int32, (tile_rows, tile_rows), 0) == lax.broadcasted_iota(
        jnp.int32, (tile_rows, tile_rows), 1
    )
    state = (
        jnp.full((HEADS, tile_rows), -1e30, jnp.float32),
        jnp.zeros((HEADS, tile_rows), jnp.float32),
        jnp.zeros((tile_rows, HEADS, HEAD_DIM), jnp.float32),
    )
    state = attend_block(state, query_heads, kv_own, (masks[REACH] > 0) | diagonal)
    latest = {1: kv_own, -1: kv_own}
    for distance in range(1, REACH + 1):
        for sign in (1, -1):
            offset = sign * distance
            source = latest[sign]
            hop = -sign
            received = passed_along(source, "blk", hop)
            latest[sign] = received
            state = attend_block(state, query_heads, received, masks[offset + REACH] > 0)
    running_top, running_total, running_sum = state
    mixed = (
        (running_sum / jnp.transpose(running_total)[:, :, None])
        .reshape(tile_rows, D)
        .astype(jnp.bfloat16)
    )
    after = xfull + jnp.dot(mixed, w_out, preferred_element_type=jnp.float32)
    count = tile_rows * lax.axis_size("blk")
    sums, squares = lax.psum((jnp.sum(after, axis=0), jnp.sum(after * after, axis=0)), "blk")
    mean = sums / count
    var = squares / count - mean * mean
    centered = after - mean
    batched = (centered * lax.rsqrt(var + 1e-05) * bn_gain + bn_shift).astype(jnp.bfloat16)
    hidden = jax.nn.gelu(
        jnp.dot(batched, w_up, preferred_element_type=jnp.float32), approximate=True
    ).astype(jnp.bfloat16)
    return (after + jnp.dot(hidden, w_down, preferred_element_type=jnp.float32)).astype(
        jnp.bfloat16
    )


def solution(mesh):
    placed = (
        P(("grp", "blk"), None),
        P(("grp", "blk"), None, None, None),
        P(),
        P(),
        P(),
        P(),
        P(),
        P(),
        P(),
        P(),
        P(),
    )
    return jax.shard_map(
        body, mesh=mesh, in_specs=placed, out_specs=P(("grp", "blk"), None), check_vma=False
    )
```

profile of v0, /device:TPU:0, one launch (start us, length us, event | category | flops | bytes accessed | tf_op | source)
XLA Modules:
  0.0 135.1 jit_solution(12724291372770317268)
XLA Ops:
  0.0 1.4 %fusion.81 = f32[512]{0:T(512)S(1)} fusion(bf16[512,512]{1,0:T(8,128)(2,1)} %param.11), kind=kLoop, calls=%fused_computation.66 | loop fusion | flops 785920 | bytes 526336 | tf_op jit(solution)/shard_map/reduce_sum | solution.py:50
  1.4 2.2 %convolution_convert_fusion.1 = bf16[512,512]{0,1:T(8,128)(2,1)S(1)} fusion(bf16[512,512]{1,0:T(8,128)(2,1)} %param.15, bf16[512,512]{1,0:T(8,128)(2,1)} %param.11, f32[512]{0:T(512)} %param.13, f32[512]{0:T(512)S(1)} %add_rsqrt_fusion.1), kind=kOutput, calls=%fused_computation.64 | convolution fusion | flops 269746176 | bytes 1576960 | tf_op jit(solution)/shard_map/dot_general | solution.py:39
  3.6 1.8 %convolution_convert_fusion = bf16[512,512]{0,1:T(8,128)(2,1)S(1)} fusion(bf16[512,512]{1,0:T(8,128)(2,1)} %param.16, bf16[512,512]{1,0:T(8,128)(2,1)} %param.11, f32[512]{0:T(512)} %param.13, f32[512]{0:T(512)S(1)} %add_rsqrt_fusion.1), kind=kOutput, calls=%fused_computation.63 | convolution fusion | flops 269746176 | bytes 1576960 | tf_op jit(solution)/shard_map/dot_general | solution.py:40
  5.4 1.2 pad_maximum_fusion
  6.6 0.5 collective-permute-start.1
  7.1 5.0 %collective-permute-start = (bf16[2,512,512]{1,2,0:T(8,128)(2,1)}, bf16[2,512,512]{1,2,0:T(8,128)(2,1)}, u32[]{:S(2)}, u32[]{:S(2)}) collective-permute-start(bf16[2,512,512]{1,2,0:T(8,128)(2,1)} %pad_maximum_fusion), channel_id=1, source_target_pairs={{0,15},{1,0},{2,1},{3,2},{4,3},{5,4},{6,5},{7,6},{8,7},{9,8},{10,9... | collective-permute-start | bytes 3145736 | tf_op jit(solution)/shard_map/ppermute | solution.py:15
  12.1 0.5 fusion.90
  13.2 0.4 copy.14
  14.0 0.4 copy.20
  14.8 1.8 %convolution_convert_fusion.2 = bf16[512,512]{0,1:T(8,128)(2,1)S(1)} fusion(bf16[512,512]{1,0:T(8,128)(2,1)} %param.14, bf16[512,512]{1,0:T(8,128)(2,1)} %param.11, f32[512]{0:T(512)S(1)} %copy-done.7, f32[512]{0:T(512)S(1)} %add_rsqrt_fusion.1), kind=kOutput, calls=%fused_computation.65 | convolution fusion | flops 269746176 | bytes 1576960 | tf_op jit(solution)/shard_map/dot_general | solution.py:52
  16.6 1.5 %fusion = (f32[8,512]{1,0:T(8,128)S(1)}, f32[8,512,512]{1,2,0:T(8,128)S(1)}) fusion(pred[512,512]{0,1:T(8,128)(4,1)S(1)} %copy.12, bf16[512,8,64]{0,2,1:T(8,128)(2,1)S(1)} %bitcast.174, bf16[512,8,64]{0,2,1:T(8,128)(2,1)S(1)} %bitcast.180), kind=kOutput, calls=%fused_computation.10 | convolution fusion | flops 274722816 | bytes 9715712 | tf_op jit(solution)/shard_map/qhd,khd->hqk/dot_general | solution.py:23
  18.1 6.9 %collective-permute-done.1 = bf16[2,512,512]{1,2,0:T(8,128)(2,1)} collective-permute-done((bf16[2,512,512]{1,2,0:T(8,128)(2,1)}, bf16[2,512,512]{1,2,0:T(8,128)(2,1)}, u32[]{:S(2)}, u32[]{:S(2)}) %collective-permute-start.1) | collective-permute-done | bytes 1048608 | tf_op jit(solution)/shard_map/ppermute | solution.py:15
  25.0 8.0 %collective-permute-start.3 = (bf16[2,512,512]{1,2,0:T(8,128)(2,1)}, bf16[2,512,512]{1,2,0:T(8,128)(2,1)S(1)}, u32[]{:S(2)}, u32[]{:S(2)}) collective-permute-start(bf16[2,512,512]{1,2,0:T(8,128)(2,1)} %collective-permute-done.1), channel_id=1, source_target_pairs={{0,1},{1,2},{2,3},{3,4},{4,5},{5,6},{6,7},{7,8},{8,9},{9,10},{10,1... | collective-permute-start | bytes 3145736 | tf_op jit(solution)/shard_map/ppermute | solution.py:15
  33.0 2.1 %fusion.137 = (bf16[1,512,512]{1,2,0:T(8,128)(2,1)}, bf16[1,512,512]{1,2,0:T(8,128)(2,1)S(1)}) fusion(bf16[2,512,512]{1,2,0:T(8,128)(2,1)} %collective-permute-done.1), kind=kLoop, calls=%fused_computation.137 | loop fusion | bytes 2097152 | tf_op jit(solution)/shard_map/slice | solution.py:22
  35.1 1.3 fusion.136
  36.4 1.5 %fusion.1 = (f32[8,512]{1,0:T(8,128)S(1)}, f32[8,512,512]{1,2,0:T(8,128)S(1)}) fusion(pred[512,512]{0,1:T(8,128)(4,1)S(1)} %copy.14, bf16[512,8,64]{0,2,1:T(8,128)(2,1)S(1)} %bitcast.175, bf16[512,8,64]{0,2,1:T(8,128)(2,1)S(1)} %bitcast.184), kind=kOutput, calls=%fused_computation.11 | convolution fusion | flops 274722816 | bytes 9715712 | tf_op jit(solution)/shard_map/qhd,khd->hqk/dot_general | solution.py:23
  37.9 4.7 %fusion.2 = (f32[8,512]{1,0:T(8,128)S(1)}, f32[8,512,512]{1,2,0:T(8,128)}) fusion(pred[512,512]{0,1:T(8,128)(4,1)S(1)} %copy.16, bf16[512,8,64]{0,2,1:T(8,128)(2,1)S(1)} %bitcast.176, bf16[512,8,64]{0,2,1:T(8,128)(2,1)S(1)} %bitcast.181), kind=kOutput, calls=%fused_computation.12 | convolution fusion | flops 274722816 | bytes 9715712 | tf_op jit(solution)/shard_map/qhd,khd->hqk/dot_general | solution.py:23
  42.6 6.5 %collective-permute-done.2 = bf16[2,512,512]{1,2,0:T(8,128)(2,1)S(1)} collective-permute-done((bf16[2,512,512]{1,2,0:T(8,128)(2,1)}, bf16[2,512,512]{1,2,0:T(8,128)(2,1)S(1)}, u32[]{:S(2)}, u32[]{:S(2)}) %collective-permute-start.2) | collective-permute-done | bytes 1048608 | tf_op jit(solution)/shard_map/ppermute | solution.py:15
  49.2 1.5 %fusion.3 = (f32[8,512]{1,0:T(8,128)S(1)}, f32[8,512,512]{1,2,0:T(8,128)S(1)}) fusion(pred[512,512]{0,1:T(8,128)(4,1)S(1)} %copy.18, bf16[512,8,64]{0,2,1:T(8,128)(2,1)S(1)} %bitcast.177, bf16[512,8,64]{0,2,1:T(8,128)(2,1)S(1)} %bitcast.183), kind=kOutput, calls=%fused_computation.13 | convolution fusion | flops 274722816 | bytes 9715712 | tf_op jit(solution)/shard_map/qhd,khd->hqk/dot_general | solution.py:23
  50.7 0.9 fusion.138
  51.6 4.7 %fusion.4 = (f32[8,512]{1,0:T(8,128)S(1)}, f32[8,512,512]{1,2,0:T(8,128)}) fusion(pred[512,512]{0,1:T(8,128)(4,1)S(1)} %copy.20, bf16[512,8,64]{0,2,1:T(8,128)(2,1)S(1)} %bitcast.178, bf16[512,8,64]{0,2,1:T(8,128)(2,1)S(1)} %bitcast.182), kind=kOutput, calls=%fused_computation.14 | convolution fusion | flops 274722816 | bytes 9715712 | tf_op jit(solution)/shard_map/qhd,khd->hqk/dot_general | solution.py:23
  56.3 5.1 %fusion.13 = f32[8,512]{1,0:T(8,128)S(1)} fusion(f32[8,512,512]{1,2,0:T(8,128)} %get-tuple-element.35, f32[8,512]{1,0:T(8,128)S(1)} %get-tuple-element.13, pred[512,512]{0,1:T(8,128)(4,1)S(1)} %copy.20), kind=kLoop, calls=%fused_computation.23 | loop fusion | flops 8384512 | bytes 8683520 | tf_op jit(solution)/shard_map/reduce_sum | solution.py:30
  61.4 5.8 %fusion.50 = f32[512,8,64]{0,2,1:T(8,128)S(1)} fusion(bf16[512,8,64]{0,2,1:T(8,128)(2,1)} %bitcast.190, f32[8,512,512]{1,2,0:T(8,128)} %get-tuple-element.35, f32[8,512]{1,0:T(8,128)S(1)} %get-tuple-element.13, pred[512,512]{0,1:T(8,128)(4,1)S(1)} %copy.20), kind=kOutput, calls=%fused_computation.51 | convolution fusion | flops 276824064 | bytes 10240000 | tf_op jit(solution)/shard_map/hqk,khd->qhd/dot_general | solution.py:31
  67.2 5.6 %fusion.44 = f32[512,8,64]{0,2,1:T(8,128)S(1)} fusion(bf16[512,8,64]{0,2,1:T(8,128)(2,1)S(1)} %bitcast.189, f32[8,512,512]{1,2,0:T(8,128)} %get-tuple-element.39, f32[8,512]{1,0:T(8,128)S(1)} %get-tuple-element.15, pred[512,512]{0,1:T(8,128)(4,1)S(1)} %copy.16), kind=kOutput, calls=%fused_computation.49 | convolution fusion | flops 276824064 | bytes 10240000 | tf_op jit(solution)/shard_map/hqk,khd->qhd/dot_general | solution.py:31
  72.7 5.9 %fusion.9 = (f32[8,512]{1,0:T(8,128)S(1)}, f32[8,512]{1,0:T(8,128)S(1)}) fusion(f32[8,512,512]{1,2,0:T(8,128)} %get-tuple-element.39, f32[8,512]{1,0:T(8,128)S(1)} %get-tuple-element.15, pred[512,512]{0,1:T(8,128)(4,1)S(1)} %copy.16, f32[8,512]{1,0:T(8,128)S(1)} %get-tuple-element.14, f32[8,512,512]{1,2,0:T(8,128)S(1)} %get-tuple-element.37, ...), kind=kLoop, calls=%fused_computation.19 | loop fusion | flops 16769024 | bytes 17367040 | tf_op jit(solution)/shard_map/reduce_sum | solution.py:30
  78.7 3.5 %fusion.5 = (f32[8,512]{1,0:T(8,128)S(1)}, f32[8,512]{1,0:T(8,128)S(1)}) fusion(f32[8,512,512]{1,2,0:T(8,128)S(1)} %get-tuple-element.43, f32[8,512]{1,0:T(8,128)S(1)} %get-tuple-element.31, pred[512,512]{0,1:T(8,128)(4,1)S(1)} %copy.12, f32[8,512]{1,0:T(8,128)S(1)} %get-tuple-element.16, f32[8,512,512]{1,2,0:T(8,128)S(1)} %get-tuple-element.41, ...), kind=kLoop, calls=%fused_computation.15 | loop fusion | flops 16769024 | bytes 17367040 | tf_op jit(solution)/shard_map/reduce_sum | solution.py:30
  82.2 2.3 %fusion.62 = f32[512,8,64]{0,2,1:T(8,128)S(1)} fusion(bf16[512,8,64]{0,2,1:T(8,128)(2,1)S(1)} %bitcast.186, f32[8,512,512]{1,2,0:T(8,128)S(1)} %get-tuple-element.43, f32[8,512]{1,0:T(8,128)S(1)} %get-tuple-element.31, pred[512,512]{0,1:T(8,128)(4,1)S(1)} %copy.12, f32[512,8]{0,1:T(8,128)S(1)} %get-tuple-element.29, f32[512,8]{0,1:T(8,128)S(1)} %get-tuple-element.30), kind=kOutput, calls=%fused_computation.56 | convolution fusion | flops 277348352 | bytes 10272768 | tf_op jit(solution)/shard_map/hqk,khd->qhd/dot_general | solution.py:31
  84.5 2.4 %fusion.71 = f32[512,8,64]{0,2,1:T(8,128)S(1)} fusion(f32[512,8,64]{0,2,1:T(8,128)S(1)} %fusion.44, f32[512,8,64]{0,2,1:T(8,128)S(1)} %fusion.62, bf16[512,8,64]{0,2,1:T(8,128)(2,1)S(1)} %bitcast.187, f32[8,512,512]{1,2,0:T(8,128)S(1)} %get-tuple-element.41, f32[8,512]{1,0:T(8,128)S(1)} %get-tuple-element.16, pred[512,512]{0,1:T(8,128)(4,1)S(1)} %copy.14, ...), kind=kOutput, calls=%fused_computation.59 | convolution fusion | flops 277872640 | bytes 12369920 | tf_op jit(solution)/shard_map/hqk,khd->qhd/dot_general | solution.py:31
  87.0 2.5 %divide_convert_fusion = bf16[512,8,64]{0,2,1:T(8,128)(2,1)S(1)} fusion(f32[512,8,64]{0,2,1:T(8,128)S(1)} %fusion.50, f32[512,8,64]{0,2,1:T(8,128)S(1)} %fusion.71, bf16[512,8,64]{0,2,1:T(8,128)(2,1)S(1)} %bitcast.188, f32[8,512,512]{1,2,0:T(8,128)S(1)} %get-tuple-element.37, f32[8,512]{1,0:T(8,128)S(1)} %get-tuple-element.14, ...), kind=kOutput, calls=%fused_computation.75 | convolution fusion | flops 278134784 | bytes 11845632 | tf_op jit(solution)/shard_map/hqk,khd->qhd/dot_general | solution.py:31
  89.5 0.5 fusion.131
  90.0 41.6 %all-reduce = (f32[512]{0:T(512)S(1)}, f32[512]{0:T(512)S(1)}) all-reduce(f32[512]{0:T(512)S(1)} %get-tuple-element.6, f32[512]{0:T(512)S(1)} %get-tuple-element.5), channel_id=1, replica_groups=mesh['grp'=2,'blk'=16] {'blk'}, use_global_device_ids=true, to_apply=%region_14.15 | all-reduce | flops 1024 | bytes 8192 | tf_op jit(solution)/shard_map/psum | solution.py:82
  131.6 3.5 %fusion.80 = bf16[512,512]{1,0:T(8,128)(2,1)} fusion(f32[512,512]{1,0:T(8,128)S(1)} %get-tuple-element.44, bf16[1024,512]{1,0:T(8,128)(2,1)S(1)} %copy-done, bf16[512,1024]{1,0:T(8,128)(2,1)} %param.20, f32[512]{0:T(512)S(1)} %copy-done.8, f32[512]{0:T(512)S(1)} %copy-done.9, f32[512]{0:T(512)S(1)} %get-tuple-element.33, f32[512]{0:T(512)S(1)} %get-tuple-element.32), kind=kOutput, calls=%fused_computation.62 | convolution fusion | flops 1080295424 | bytes 3678208 | tf_op jit(solution)/shard_map/dot_general | solution.py:90
  (32 shorter events, 1.5 us)
Async XLA Ops:
  0.0 131.6 %copy-start = (bf16[1024,512]{1,0:T(8,128)(2,1)S(1)}, bf16[1024,512]{1,0:T(8,128)(2,1)}, u32[]{:S(2)}) copy-start(bf16[1024,512]{1,0:T(8,128)(2,1)} %param.21) | copy-start | bytes 3145732
  0.0 14.8 %copy-start.7 = (f32[512]{0:T(512)S(1)}, f32[512]{0:T(512)}, u32[]{:S(2)}) copy-start(f32[512]{0:T(512)} %param.13) | copy-start | bytes 6148
  0.0 12.1 %copy-start.1 = (s32[1,5,512,512]{3,2,1,0:T(8,128)S(1)}, s32[1,5,512,512]{3,2,1,0:T(8,128)}, u32[]{:S(2)}) copy-start(s32[1,5,512,512]{3,2,1,0:T(8,128)} %param.12) | copy-start | bytes 15728644
  5.4 1.7 %copy-start.3 = (bf16[512,512]{0,1:T(8,128)(2,1)}, bf16[512,512]{0,1:T(8,128)(2,1)S(1)}, u32[]{:S(2)}) copy-start(bf16[512,512]{0,1:T(8,128)(2,1)S(1)} %convolution_convert_fusion) | copy-start | bytes 1572868
  6.6 18.4 %collective-permute-start.1 = (bf16[2,512,512]{1,2,0:T(8,128)(2,1)}, bf16[2,512,512]{1,2,0:T(8,128)(2,1)}, u32[]{:S(2)}, u32[]{:S(2)}) collective-permute-start(bf16[2,512,512]{1,2,0:T(8,128)(2,1)} %pad_maximum_fusion), channel_id=1, source_target_pairs={{0,1},{1,2},{2,3},{3,4},{4,5},{5,6},{6,7},{7,8},{8,9},{9,10},{10,1... | collective-permute-start | bytes 3145736 | tf_op jit(solution)/shard_map/ppermute | solution.py:15
  7.1 28.0 %collective-permute-start = (bf16[2,512,512]{1,2,0:T(8,128)(2,1)}, bf16[2,512,512]{1,2,0:T(8,128)(2,1)}, u32[]{:S(2)}, u32[]{:S(2)}) collective-permute-start(bf16[2,512,512]{1,2,0:T(8,128)(2,1)} %pad_maximum_fusion), channel_id=1, source_target_pairs={{0,15},{1,0},{2,1},{3,2},{4,3},{5,4},{6,5},{7,6},{8,7},{9,8},{10,9... | collective-permute-start | bytes 3145736 | tf_op jit(solution)/shard_map/ppermute | solution.py:15
  25.0 25.7 %collective-permute-start.3 = (bf16[2,512,512]{1,2,0:T(8,128)(2,1)}, bf16[2,512,512]{1,2,0:T(8,128)(2,1)S(1)}, u32[]{:S(2)}, u32[]{:S(2)}) collective-permute-start(bf16[2,512,512]{1,2,0:T(8,128)(2,1)} %collective-permute-done.1), channel_id=1, source_target_pairs={{0,1},{1,2},{2,3},{3,4},{4,5},{5,6},{6,7},{7,8},{8,9},{9,10},{10,1... | collective-permute-start | bytes 3145736 | tf_op jit(solution)/shard_map/ppermute | solution.py:15
  35.1 14.0 %collective-permute-start.2 = (bf16[2,512,512]{1,2,0:T(8,128)(2,1)}, bf16[2,512,512]{1,2,0:T(8,128)(2,1)S(1)}, u32[]{:S(2)}, u32[]{:S(2)}) collective-permute-start(bf16[2,512,512]{1,2,0:T(8,128)(2,1)} %collective-permute-done), channel_id=1, source_target_pairs={{0,15},{1,0},{2,1},{3,2},{4,3},{5,4},{6,5},{7,6},{8,7},{9,8},{10,9... | collective-permute-start | bytes 3145736 | tf_op jit(solution)/shard_map/ppermute | solution.py:15
  61.4 5.8 %copy-start.5 = (bf16[1,512,512]{1,2,0:T(8,128)(2,1)S(1)}, bf16[1,512,512]{1,2,0:T(8,128)(2,1)}, u32[]{:S(2)}) copy-start(bf16[1,512,512]{1,2,0:T(8,128)(2,1)} %get-tuple-element.25) | copy-start | bytes 1572868
  78.6 3.6 %copy-start.4 = (bf16[512,512]{0,1:T(8,128)(2,1)S(1)}, bf16[512,512]{0,1:T(8,128)(2,1)}, u32[]{:S(2)}) copy-start(bf16[512,512]{0,1:T(8,128)(2,1)} %copy-done.3) | copy-start | bytes 1572868
  87.0 2.5 %copy-start.2 = (bf16[512,512]{1,0:T(8,128)(2,1)S(1)}, bf16[512,512]{1,0:T(8,128)(2,1)}, u32[]{:S(2)}) copy-start(bf16[512,512]{1,0:T(8,128)(2,1)} %param.11) | copy-start | bytes 1572868
  87.0 2.5 %copy-start.6 = (bf16[512,512]{1,0:T(8,128)(2,1)S(1)}, bf16[512,512]{1,0:T(8,128)(2,1)}, u32[]{:S(2)}) copy-start(bf16[512,512]{1,0:T(8,128)(2,1)} %param.17) | copy-start | bytes 1572868
  87.0 44.6 %copy-start.8 = (f32[512]{0:T(512)S(1)}, f32[512]{0:T(512)}, u32[]{:S(2)}) copy-start(f32[512]{0:T(512)} %param.19) | copy-start | bytes 6148
  87.0 44.6 %copy-start.9 = (f32[512]{0:T(512)S(1)}, f32[512]{0:T(512)}, u32[]{:S(2)}) copy-start(f32[512]{0:T(512)} %param.18) | copy-start | bytes 6148
where the time goes:
time: 135 us
  matrix products  42.3 us (31%)
  blocking collectives  41.6 us (31%)
  other arithmetic  17.8 us (13%)
  starting transfers between devices  13.5 us (10%)
  waiting for transfers between devices  13.3 us (10%)
  local copies, waits for them, and re-layouts  6.33 us (5%)
    psum x1, blocking collectives, body(): lax.psum((jnp.sum(after, axis=0), jnp.sum(after * after, axis=0)), 'blk')  41.6 us
    dot_general x5, matrix products, attend_block(): jnp.einsum('hqk,khd->qhd', expo.astype(jnp.bfloat16), value_heads, prefer...  18.5 us
    reduce_sum x3, other arithmetic, attend_block(): new_total = running_total * factor + jnp.sum(expo, axis=-1)  14.5 us
    dot_general x5, matrix products, attend_block(): jnp.einsum('qhd,khd->hqk', query_heads, key_heads, preferred_element_type...  14 us
    ppermute x4, starting transfers between devices, passed_along(): return lax.ppermute(value, axis, pairs)  13.5 us
    ppermute x4, waiting for transfers between devices, passed_along(): return lax.ppermute(value, axis, pairs)  13.3 us
    dot_general x1, matrix products, body(): jnp.dot(hidden, w_down, preferred_element_type=jnp.float32)  3.47 us
    slice x3, local copies, waits for them, and re-layouts, attend_block(): value_heads = kv_block[1].reshape(tile_rows, HEADS, HEAD_DIM)  3.41 us
  transfers between devices with their start and end apart: 4, of which 2 were waited for; matrix products, arithmetic and copies ran while one was open for 13% of the time, Pallas kernels for 0%

commit v1 on v0

v1 whole, which is shorter than its diff:
```python
import functools

import jax
import jax.numpy as jnp
from jax import lax
from jax.experimental import pallas as pl
from jax.experimental.pallas import tpu as pltpu
from jax.sharding import PartitionSpec as P

HEAD_DIM = 64
PAIR = 2 * HEAD_DIM
REACH = 2
CHUNKS = 4
NEG = -1e30
MESH = pl.DeviceIdType.MESH
PARTNER, MIRROR, RAIL, CROSS = 0, 1, 2, 3
ROWS_STEP = 256


def kernel(
    n,
    atoms_hbm, mask_hbm, ng_hbm, wq_hbm, wk_hbm, wv_hbm, wo_hbm, bg_hbm, bs_hbm, wu_hbm, wd_hbm,
    out_ref,
    x_ref, mask_ref, ng_ref, wq_ref, wk_ref, wv_ref, wo_ref, bg_ref, bs_ref, wu_ref, wd_ref,
    nb_ref, qm_ref, kb_ref, va_ref, bias_ref, m_ref, l_ref, acc_ref, mixed_ref, after_ref,
    stats_ref, load_sem, mask_sem,
    p_send, p_recv, m_send, m_recv, r_send, r_recv, c_send, c_recv, s_send, s_recv,
):
    me = lax.axis_index("blk")
    rows, width = x_ref.shape
    pairs = width // PAIR
    group, inside = me // 4, me % 4
    side, core = inside // 2, inside % 2
    partner = group * 4 + side * 2 + (1 - core)
    mirror = group * 4 + (1 - side) * 2 + core
    groups = n // 4
    rail_to = ((group + 1 - 2 * side + groups) % groups) * 4 + side * 2 + core
    cross_source = jnp.where(side == core, MIRROR, RAIL)

    barrier = pltpu.get_barrier_semaphore()

    def greet(d, carry):
        pl.semaphore_signal(
            barrier, inc=1, device_id={"blk": lax.rem(me + d, n)}, device_id_type=MESH
        )
        return carry

    lax.fori_loop(1, n, greet, 0)

    sources = (
        (atoms_hbm, x_ref), (ng_hbm, ng_ref), (wq_hbm, wq_ref), (wk_hbm, wk_ref), (wv_hbm, wv_ref),
        (wo_hbm, wo_ref), (bg_hbm, bg_ref), (bs_hbm, bs_ref), (wu_hbm, wu_ref), (wd_hbm, wd_ref),
    )
    loads = [
        pltpu.make_async_copy(src, dst, load_sem.at[i]) for i, (src, dst) in enumerate(sources)
    ]

    far = jnp.where(side == 0, 2, -2)
    near = jnp.where(core == 0, 1, -1)
    offsets = [jnp.int32(0), near, far, -far, -near]
    masks = [
        pltpu.make_async_copy(
            mask_hbm.at[0, offsets[i] + REACH], mask_ref.at[i], mask_sem.at[i]
        )
        for i in range(2 * REACH + 1)
    ]
    for i in range(5):
        loads[i].start()
    for mask_load in masks:
        mask_load.start()
    for i in range(5, len(loads)):
        loads[i].start()

    step_rows = rows // CHUNKS

    def chunk(c):
        return pl.ds(c * step_rows, step_rows)

    def mirror_copy(c):
        return pltpu.make_async_remote_copy(
            src_ref=x_ref.at[chunk(c)], dst_ref=nb_ref.at[MIRROR, chunk(c)],
            send_sem=m_send.at[c], recv_sem=m_recv.at[c],
            device_id={"blk": mirror}, device_id_type=MESH,
        )

    def rail_copy(c):
        return pltpu.make_async_remote_copy(
            src_ref=nb_ref.at[MIRROR, chunk(c)], dst_ref=nb_ref.at[RAIL, chunk(c)],
            send_sem=r_send.at[c], recv_sem=r_recv.at[c],
            device_id={"blk": rail_to}, device_id_type=MESH,
        )

    def cross_copy(c):
        return pltpu.make_async_remote_copy(
            src_ref=nb_ref.at[cross_source, chunk(c)], dst_ref=nb_ref.at[CROSS, chunk(c)],
            send_sem=c_send.at[c], recv_sem=c_recv.at[c],
            device_id={"blk": partner}, device_id_type=MESH,
        )

    partner_copy = pltpu.make_async_remote_copy(
        src_ref=x_ref, dst_ref=nb_ref.at[PARTNER], send_sem=p_send, recv_sem=p_recv,
        device_id={"blk": partner}, device_id_type=MESH,
    )

    def relay_rail(c):
        mirror_copy(c).wait_recv()
        rail_copy(c).start()

    def relay_cross(c):
        rail_copy(c).wait_recv()
        cross_copy(c).start()

    loads[0].wait()
    pl.semaphore_wait(barrier, n - 1)
    for c in range(CHUNKS):
        mirror_copy(c).start()
    partner_copy.start()

    def normalize(value):
        full = value.astype(jnp.float32)
        return (
            full * lax.rsqrt(jnp.mean(full * full, axis=-1, keepdims=True) + 1e-06) * ng_ref[...]
        ).astype(jnp.bfloat16)

    left = lax.broadcasted_iota(jnp.int32, (rows, PAIR), 1) < HEAD_DIM
    left_step = lax.broadcasted_iota(jnp.int32, (ROWS_STEP, PAIR), 1) < HEAD_DIM

    for h in range(pairs):
        va_ref[h, :, PAIR:] = jnp.ones((rows, PAIR), jnp.bfloat16)

    def set_keys(normed):
        keys = jnp.dot(normed, wk_ref[...], preferred_element_type=jnp.float32).astype(jnp.bfloat16)
        values = jnp.dot(normed, wv_ref[...], preferred_element_type=jnp.float32).astype(jnp.bfloat16)
        for h in range(pairs):
            kb_ref[h] = keys[:, h * PAIR:(h + 1) * PAIR]
            va_ref[h, :, :PAIR] = values[:, h * PAIR:(h + 1) * PAIR]

    def attend(i, first, between):
        masks[i].wait()
        allowed = mask_ref[i] > 0
        if i == 0:
            allowed = allowed | (
                lax.broadcasted_iota(jnp.int32, (rows, rows), 0)
                == lax.broadcasted_iota(jnp.int32, (rows, rows), 1)
            )
        bias_ref[...] = jnp.where(allowed, 0.0, NEG)

        def one_pair(h, carry):
            keys = kb_ref[h]
            values = va_ref[h]
            for r in range(0, rows, ROWS_STEP):
                piece = pl.ds(r, ROWS_STEP)
                results = []
                for j in range(2):
                    score = lax.dot_general(
                        qm_ref[2 * h + j, piece], keys, (((1,), (1,)), ((), ())),
                        preferred_element_type=jnp.float32,
                    ) + bias_ref[piece]
                    top = jnp.max(score, axis=-1, keepdims=True)
                    if first:
                        m_ref[2 * h + j, piece] = jnp.broadcast_to(top, (ROWS_STEP, PAIR))
                        factor = None
                    else:
                        old = m_ref[2 * h + j, piece]
                        new = jnp.maximum(old, top)
                        factor = jnp.exp(old - new)
                        m_ref[2 * h + j, piece] = new
                        top = new[:, :1]
                    weight = jnp.exp(score - top).astype(jnp.bfloat16)
                    product = jnp.dot(weight, values, preferred_element_type=jnp.float32)
                    results.append((factor, product))
                (fa, a), (fb, b) = results
                mixed = jnp.where(left_step, a[:, :PAIR], b[:, :PAIR])
                total = jnp.where(left_step, a[:, PAIR:], b[:, PAIR:])
                if first:
                    acc_ref[h, piece] = mixed
                    l_ref[h, piece] = total
                else:
                    factor = jnp.where(left_step, fa, fb)
                    acc_ref[h, piece] = acc_ref[h, piece] * factor + mixed
                    l_ref[h, piece] = l_ref[h, piece] * factor + total
            between(h)
            return carry

        lax.fori_loop(0, pairs, one_pair, 0)

    def at_odd(relay, base):
        def run(h):
            @pl.when(lax.rem(h, 2) == 1)
            def _():
                relay(base + h // 2)
        return run

    def nothing(h):
        pass

    loads[1].wait()
    normed = normalize(x_ref[...])
    loads[2].wait()
    query = jnp.dot(normed, wq_ref[...], preferred_element_type=jnp.float32).astype(jnp.bfloat16)
    query = query * jnp.bfloat16(HEAD_DIM ** (-0.5))
    zero = jnp.zeros((rows, PAIR), jnp.bfloat16)
    for h in range(pairs):
        piece = query[:, h * PAIR:(h + 1) * PAIR]
        qm_ref[2 * h] = jnp.where(left, piece, zero)
        qm_ref[2 * h + 1] = jnp.where(left, zero, piece)
    loads[3].wait()
    loads[4].wait()
    set_keys(normed)
    attend(0, True, at_odd(relay_rail, 0))

    partner_copy.wait_recv()
    set_keys(normalize(nb_ref[PARTNER]))
    attend(1, False, at_odd(relay_rail, 2))

    set_keys(normalize(nb_ref[MIRROR]))
    attend(2, False, at_odd(relay_cross, 0))

    for c in range(CHUNKS // 2, CHUNKS):
        relay_cross(c)
    set_keys(normalize(nb_ref[RAIL]))
    attend(3, False, nothing)

    for c in range(CHUNKS):
        cross_copy(c).wait_recv()
    set_keys(normalize(nb_ref[CROSS]))
    attend(4, False, nothing)

    for h in range(pairs):
        mixed_ref[:, h * PAIR:(h + 1) * PAIR] = (acc_ref[h] / l_ref[h]).astype(jnp.bfloat16)
    for load in loads[5:]:
        load.wait()
    after_ref[...] = x_ref[...].astype(jnp.float32) + jnp.dot(
        mixed_ref[...], wo_ref[...], preferred_element_type=jnp.float32
    )

    local_mean = jnp.sum(after_ref[...], axis=0, keepdims=True) * (1.0 / rows)
    spread = after_ref[...] - local_mean
    stats_ref[0, 0:1] = local_mean
    stats_ref[0, 1:2] = jnp.sum(spread * spread, axis=0, keepdims=True)

    def stats_copy(d):
        return pltpu.make_async_remote_copy(
            src_ref=stats_ref.at[0], dst_ref=stats_ref.at[d],
            send_sem=s_send.at[d], recv_sem=s_recv.at[d],
            device_id={"blk": lax.rem(me + d, n)}, device_id_type=MESH,
        )

    def send_stats(d, carry):
        stats_copy(d).start()
        return carry

    def take_stats(d, carry):
        stats_copy(d).wait_recv()
        return carry

    lax.fori_loop(1, n, send_stats, 0)

    partner_copy.wait_send()
    for c in range(CHUNKS):
        mirror_copy(c).wait_send()
        rail_copy(c).wait_send()
        cross_copy(c).wait_send()

    lax.fori_loop(1, n, take_stats, 0)
    gathered = stats_ref[...]
    means = gathered[:, 0, :]
    mean = jnp.sum(means, axis=0, keepdims=True) * (1.0 / n)
    shifts = means - mean
    var = (
        jnp.sum(gathered[:, 1, :], axis=0, keepdims=True) * (1.0 / rows)
        + jnp.sum(shifts * shifts, axis=0, keepdims=True)
    ) * (1.0 / n)
    gain = lax.rsqrt(var + 1e-05) * bg_ref[...]
    batched = ((after_ref[...] - mean) * gain + bs_ref[...]).astype(jnp.bfloat16)
    hidden = jax.nn.gelu(
        jnp.dot(batched, wu_ref[...], preferred_element_type=jnp.float32), approximate=True
    ).astype(jnp.bfloat16)
    out_ref[...] = (
        after_ref[...] + jnp.dot(hidden, wd_ref[...], preferred_element_type=jnp.float32)
    ).astype(jnp.bfloat16)

    def sent_stats(d, carry):
        stats_copy(d).wait_send()
        return carry

    lax.fori_loop(1, n, sent_stats, 0)


def body(
    atoms, edge_mask, norm_gain, w_query, w_key, w_value, w_out, bn_gain, bn_shift, w_up, w_down
):
    n = lax.axis_size("blk")
    rows, width = atoms.shape
    ff = w_up.shape[1]
    slabs = edge_mask.shape[1]
    pairs = width // PAIR
    bf16, f32 = jnp.bfloat16, jnp.float32
    dma = pltpu.SemaphoreType.DMA
    return pl.pallas_call(
        functools.partial(kernel, n),
        out_shape=jax.ShapeDtypeStruct((rows, width), bf16),
        in_specs=[pl.BlockSpec(memory_space=pl.ANY)] * 11,
        out_specs=pl.BlockSpec(memory_space=pltpu.VMEM),
        scratch_shapes=[
            pltpu.VMEM((rows, width), bf16),
            pltpu.VMEM((slabs, rows, rows), jnp.int32),
            pltpu.VMEM((1, width), f32),
            pltpu.VMEM((width, width), bf16),
            pltpu.VMEM((width, width), bf16),
            pltpu.VMEM((width, width), bf16),
            pltpu.VMEM((width, width), bf16),
            pltpu.VMEM((1, width), f32),
            pltpu.VMEM((1, width), f32),
            pltpu.VMEM((width, ff), bf16),
            pltpu.VMEM((ff, width), bf16),
            pltpu.VMEM((4, rows, width), bf16),
            pltpu.VMEM((2 * pairs, rows, PAIR), bf16),
            pltpu.VMEM((pairs, rows, PAIR), bf16),
            pltpu.VMEM((pairs, rows, 2 * PAIR), bf16),
            pltpu.VMEM((rows, rows), f32),
            pltpu.VMEM((2 * pairs, rows, PAIR), f32),
            pltpu.VMEM((pairs, rows, PAIR), f32),
            pltpu.VMEM((pairs, rows, PAIR), f32),
            pltpu.VMEM((rows, width), bf16),
            pltpu.VMEM((rows, width), f32),
            pltpu.VMEM((n, 2, width), f32),
            dma((10,)),
            dma((slabs,)),
            dma, dma,
            dma((CHUNKS,)), dma((CHUNKS,)),
            dma((CHUNKS,)), dma((CHUNKS,)),
            dma((CHUNKS,)), dma((CHUNKS,)),
            dma((n,)), dma((n,)),
        ],
        compiler_params=pltpu.CompilerParams(
            collective_id=0, has_side_effects=True, vmem_limit_bytes=60 * 1024 * 1024
        ),
    )(
        atoms, edge_mask, norm_gain.reshape(1, width), w_query, w_key, w_value, w_out,
        bn_gain.reshape(1, width), bn_shift.reshape(1, width), w_up, w_down,
    )


def solution(mesh):
    placed = (
        P(("grp", "blk"), None),
        P(("grp", "blk"), None, None, None),
        P(), P(), P(), P(), P(), P(), P(), P(), P(),
    )
    return jax.shard_map(
        body, mesh=mesh, in_specs=placed, out_specs=P(("grp", "blk"), None), check_vma=False
    )
```

time: 135 us -> 50 us (0.37)
  Pallas kernels: 0 us -> 47.9 us
  matrix products: 42.3 us -> 0 us
  blocking collectives: 41.6 us -> 0 us
  other arithmetic: 17.8 us -> 0 us
  starting transfers between devices: 13.5 us -> 0 us
  waiting for transfers between devices: 13.3 us -> 0 us
  local copies, waits for them, and re-layouts: 6.33 us -> 1.87 us
    pallas_call x0 -> x1, Pallas kernels: none -> 47.9 us  [body(): pl.pallas_call(functools.partial(kernel, n), out_shape=jax.ShapeDtypeStru...]
    dot_general x15 -> x0, matrix products: 42.3 us -> none  [the longest x5 18.5 us: attend_block(): jnp.einsum('hqk,khd->qhd', expo.astype(jnp.bfloat16), value_heads, prefer...]
    psum x1 -> x0, blocking collectives: 41.6 us -> none  [body(): lax.psum((jnp.sum(after, axis=0), jnp.sum(after * after, axis=0)), 'blk')]
    reduce_sum x4 -> x0, other arithmetic: 15.9 us -> none  [the longest x3 14.5 us: attend_block(): new_total = running_total * factor + jnp.sum(expo, axis=-1)]
    ppermute x4 -> x0, starting transfers between devices: 13.5 us -> none  [passed_along(): return lax.ppermute(value, axis, pairs)]
    ppermute x4 -> x0, waiting for transfers between devices: 13.3 us -> none  [passed_along(): return lax.ppermute(value, axis, pairs)]
    slice x4 -> x0, local copies, waits for them, and re-layouts: 4.27 us -> none  [the longest x3 3.41 us: attend_block(): value_heads = kv_block[1].reshape(tile_rows, HEADS, HEAD_DIM)]
    unnamed x20 -> x1, local copies, waits for them, and re-layouts: 0.05 us -> 1.87 us
  transfers between devices with their start and end apart: 4 -> 0, of which waited for: 2 -> 0; matrix products, arithmetic and copies ran while one was open for 13% -> 0% of each run, Pallas kernels for 0% -> 0%
where the time goes in v1:
time: 50 us; the launch traced here: 49.8 us
  Pallas kernels  47.9 us (96%)
  local copies, waits for them, and re-layouts  1.87 us (4%)
    pallas_call x1, Pallas kernels, body(): pl.pallas_call(functools.partial(kernel, n), out_shape=jax.ShapeDtypeStru...  47.9 us
    unnamed x1, local copies, waits for them, and re-layouts  1.87 us

profile of v1, /device:TPU:0, one launch (start us, length us, event | category | flops | bytes accessed | tf_op | source)
XLA Modules:
  0.0 49.8 jit_solution(14307448702106667465)
XLA Ops:
  0.0 47.9 %shard_map.109 = bf16[512,512]{1,0:T(8,128)(2,1)} custom-call(bf16[512,512]{1,0:T(8,128)(2,1)} %atoms_hbm.1, s32[1,5,512,512]{3,2,1,0:T(8,128)} %mask_hbm.1, f32[1,512]{1,0:T(1,128)} %bitcast.3, bf16[512,512]{1,0:T(8,128)(2,1)} %wq_hbm.1, bf16[512,512]{1,0:T(8,128)(2,1)} %wk_hbm.1, bf16[512,512]{1,0:T(8,128)(2,1)} %wv_hbm.1, bf16[512,512]{1,0:T(8,128)(2,1)} %wo_hbm.1, ...), custom_call_target="tpu_custom_call" | custom-call | tf_op jit(solution)/shard_map/pallas_call | solution.py:300
  47.9 1.9 %copy.13 = bf16[512,512]{1,0:T(8,128)(2,1)} copy(bf16[512,512]{1,0:T(8,128)(2,1)} %shard_map.109) | data formatting | bytes 1048576

commit v2 on v1

--- a/solution.py
+++ b/solution.py
@@ -14,7 +14,9 @@
 NEG = -1e30
 MESH = pl.DeviceIdType.MESH
 PARTNER, MIRROR, RAIL, CROSS = 0, 1, 2, 3
-ROWS_STEP = 256
+ROWS_STEP = 128
+UNROLL = 2
+SLOTS = 2
 
 
 def kernel(
@@ -110,12 +112,6 @@
         rail_copy(c).wait_recv()
         cross_copy(c).start()
 
-    loads[0].wait()
-    pl.semaphore_wait(barrier, n - 1)
-    for c in range(CHUNKS):
-        mirror_copy(c).start()
-    partner_copy.start()
-
     def normalize(value):
         full = value.astype(jnp.float32)
         return (
@@ -124,18 +120,20 @@
 
     left = lax.broadcasted_iota(jnp.int32, (rows, PAIR), 1) < HEAD_DIM
     left_step = lax.broadcasted_iota(jnp.int32, (ROWS_STEP, PAIR), 1) < HEAD_DIM
-
-    for h in range(pairs):
-        va_ref[h, :, PAIR:] = jnp.ones((rows, PAIR), jnp.bfloat16)
-
-    def set_keys(normed):
+    pieces = rows // ROWS_STEP
+
+    for g in range(SLOTS):
+        for h in range(pairs):
+            va_ref[g, h, :, PAIR:] = jnp.ones((rows, PAIR), jnp.bfloat16)
+
+    def set_keys(g, normed):
         keys = jnp.dot(normed, wk_ref[...], preferred_element_type=jnp.float32).astype(jnp.bfloat16)
         values = jnp.dot(normed, wv_ref[...], preferred_element_type=jnp.float32).astype(jnp.bfloat16)
         for h in range(pairs):
-            kb_ref[h] = keys[:, h * PAIR:(h + 1) * PAIR]
-            va_ref[h, :, :PAIR] = values[:, h * PAIR:(h + 1) * PAIR]
-
-    def attend(i, first, between):
+            kb_ref[g, h] = keys[:, h * PAIR:(h + 1) * PAIR]
+            va_ref[g, h, :, :PAIR] = values[:, h * PAIR:(h + 1) * PAIR]
+
+    def set_bias(g, i):
         masks[i].wait()
         allowed = mask_ref[i] > 0
         if i == 0:
@@ -143,57 +141,95 @@
                 lax.broadcasted_iota(jnp.int32, (rows, rows), 0)
                 == lax.broadcasted_iota(jnp.int32, (rows, rows), 1)
             )
-        bias_ref[...] = jnp.where(allowed, 0.0, NEG)
-
-        def one_pair(h, carry):
-            keys = kb_ref[h]
-            values = va_ref[h]
-            for r in range(0, rows, ROWS_STEP):
-                piece = pl.ds(r, ROWS_STEP)
-                results = []
-                for j in range(2):
-                    score = lax.dot_general(
-                        qm_ref[2 * h + j, piece], keys, (((1,), (1,)), ((), ())),
-                        preferred_element_type=jnp.float32,
-                    ) + bias_ref[piece]
-                    top = jnp.max(score, axis=-1, keepdims=True)
-                    if first:
-                        m_ref[2 * h + j, piece] = jnp.broadcast_to(top, (ROWS_STEP, PAIR))
-                        factor = None
-                    else:
-                        old = m_ref[2 * h + j, piece]
-                        new = jnp.maximum(old, top)
-                        factor = jnp.exp(old - new)
-                        m_ref[2 * h + j, piece] = new
-                        top = new[:, :1]
-                    weight = jnp.exp(score - top).astype(jnp.bfloat16)
-                    product = jnp.dot(weight, values, preferred_element_type=jnp.float32)
-                    results.append((factor, product))
-                (fa, a), (fb, b) = results
-                mixed = jnp.where(left_step, a[:, :PAIR], b[:, :PAIR])
-                total = jnp.where(left_step, a[:, PAIR:], b[:, PAIR:])
-                if first:
-                    acc_ref[h, piece] = mixed
-                    l_ref[h, piece] = total
-                else:
-                    factor = jnp.where(left_step, fa, fb)
-                    acc_ref[h, piece] = acc_ref[h, piece] * factor + mixed
-                    l_ref[h, piece] = l_ref[h, piece] * factor + total
-            between(h)
+        bias_ref[g] = jnp.where(allowed, 0.0, NEG)
+
+    def attend(count, first, between):
+        blocks = rows // PAIR
+
+        def scores(h, r):
+            piece = pl.ds(r * ROWS_STEP, ROWS_STEP)
+            found = []
+            peaks = [None, None]
+            for g in range(count):
+                score = lax.dot_general(
+                    qm_ref[h, r], kb_ref[g, h], (((1,), (1,)), ((), ())),
+                    preferred_element_type=jnp.float32,
+                )
+                for b in range(blocks):
+                    bias = bias_ref[g, piece, b * PAIR:(b + 1) * PAIR]
+                    both = []
+                    for j in range(2):
+                        part = score[
+                            j * ROWS_STEP:(j + 1) * ROWS_STEP, b * PAIR:(b + 1) * PAIR
+                        ] + bias
+                        peaks[j] = part if peaks[j] is None else jnp.maximum(peaks[j], part)
+                        both.append(part)
+                    found.append(both)
+            return found, peaks
+
+        def finish(h, r, found, peaks):
+            piece = pl.ds(r * ROWS_STEP, ROWS_STEP)
+            if not first:
+                old = m_ref[h, piece]
+                peaks = [
+                    jnp.maximum(peaks[0], jnp.where(left_step, old, NEG)),
+                    jnp.maximum(peaks[1], jnp.where(left_step, NEG, old)),
+                ]
+            tops = [
+                jnp.broadcast_to(jnp.max(peak, axis=-1, keepdims=True), (ROWS_STEP, PAIR))
+                for peak in peaks
+            ]
+            new = jnp.where(left_step, tops[0], tops[1])
+            m_ref[h, piece] = new
+            result = None
+            for g in range(count):
+                weight = jnp.concatenate([
+                    jnp.concatenate([
+                        jnp.exp(found[g * blocks + b][j] - tops[j]).astype(jnp.bfloat16)
+                        for b in range(blocks)
+                    ], axis=1)
+                    for j in range(2)
+                ], axis=0)
+                product = jnp.dot(weight, va_ref[g, h], preferred_element_type=jnp.float32)
+                result = product if result is None else result + product
+            mixed = jnp.where(left_step, result[:ROWS_STEP, :PAIR], result[ROWS_STEP:, :PAIR])
+            total = jnp.where(left_step, result[:ROWS_STEP, PAIR:], result[ROWS_STEP:, PAIR:])
+            if first:
+                acc_ref[h, piece] = mixed
+                l_ref[h, piece] = total
+            else:
+                factor = jnp.exp(old - new)
+                acc_ref[h, piece] = acc_ref[h, piece] * factor + mixed
+                l_ref[h, piece] = l_ref[h, piece] * factor + total
+
+        def some_pairs(t, carry):
+            units = [(t * UNROLL + u, r) for u in range(UNROLL) for r in range(pieces)]
+            ahead = scores(*units[0])
+            for k, unit in enumerate(units):
+                current = ahead
+                if k + 1 < len(units):
+                    ahead = scores(*units[k + 1])
+                finish(*unit, *current)
+            between(t)
             return carry
 
-        lax.fori_loop(0, pairs, one_pair, 0)
-
-    def at_odd(relay, base):
-        def run(h):
-            @pl.when(lax.rem(h, 2) == 1)
-            def _():
-                relay(base + h // 2)
+        lax.fori_loop(0, pairs // UNROLL, some_pairs, 0)
+
+    half = CHUNKS // 2
+
+    def each(relay, base):
+        def run(t):
+            for u in range(UNROLL):
+                h = t * UNROLL + u
+                @pl.when(lax.rem(h, 2) == 1)
+                def _():
+                    relay(base + h // 2)
         return run
 
-    def nothing(h):
+    def nothing(t):
         pass
 
+    loads[0].wait()
     loads[1].wait()
     normed = normalize(x_ref[...])
     loads[2].wait()
@@ -202,29 +238,39 @@
     zero = jnp.zeros((rows, PAIR), jnp.bfloat16)
     for h in range(pairs):
         piece = query[:, h * PAIR:(h + 1) * PAIR]
-        qm_ref[2 * h] = jnp.where(left, piece, zero)
-        qm_ref[2 * h + 1] = jnp.where(left, zero, piece)
+        first_head = jnp.where(left, piece, zero)
+        second_head = jnp.where(left, zero, piece)
+        for r in range(pieces):
+            qm_ref[h, r, :ROWS_STEP] = first_head[r * ROWS_STEP:(r + 1) * ROWS_STEP]
+            qm_ref[h, r, ROWS_STEP:] = second_head[r * ROWS_STEP:(r + 1) * ROWS_STEP]
     loads[3].wait()
     loads[4].wait()
-    set_keys(normed)
-    attend(0, True, at_odd(relay_rail, 0))
+    set_keys(0, normed)
+    pl.semaphore_wait(barrier, n - 1)
+    partner_copy.start()
+    for c in range(CHUNKS):
+        mirror_copy(c).start()
+    set_bias(0, 0)
+    attend(1, True, each(relay_rail, 0))
 
     partner_copy.wait_recv()
-    set_keys(normalize(nb_ref[PARTNER]))
-    attend(1, False, at_odd(relay_rail, 2))
-
-    set_keys(normalize(nb_ref[MIRROR]))
-    attend(2, False, at_odd(relay_cross, 0))
-
-    for c in range(CHUNKS // 2, CHUNKS):
+    set_keys(0, normalize(nb_ref[PARTNER]))
+    set_bias(0, 1)
+    attend(1, False, each(relay_rail, half))
+
+    set_keys(0, normalize(nb_ref[MIRROR]))
+    set_bias(0, 2)
+    attend(1, False, each(relay_cross, 0))
+
+    for c in range(half, CHUNKS):
         relay_cross(c)
-    set_keys(normalize(nb_ref[RAIL]))
-    attend(3, False, nothing)
-
+    set_keys(0, normalize(nb_ref[RAIL]))
+    set_bias(0, 3)
     for c in range(CHUNKS):
         cross_copy(c).wait_recv()
-    set_keys(normalize(nb_ref[CROSS]))
-    attend(4, False, nothing)
+    set_keys(1, normalize(nb_ref[CROSS]))
+    set_bias(1, 4)
+    attend(2, False, nothing)
 
     for h in range(pairs):
         mixed_ref[:, h * PAIR:(h + 1) * PAIR] = (acc_ref[h] / l_ref[h]).astype(jnp.bfloat16)
@@ -315,11 +361,11 @@
             pltpu.VMEM((width, ff), bf16),
             pltpu.VMEM((ff, width), bf16),
             pltpu.VMEM((4, rows, width), bf16),
-            pltpu.VMEM((2 * pairs, rows, PAIR), bf16),
-            pltpu.VMEM((pairs, rows, PAIR), bf16),
-            pltpu.VMEM((pairs, rows, 2 * PAIR), bf16),
-            pltpu.VMEM((rows, rows), f32),
-            pltpu.VMEM((2 * pairs, rows, PAIR), f32),
+            pltpu.VMEM((pairs, rows // ROWS_STEP, 2 * ROWS_STEP, PAIR), bf16),
+            pltpu.VMEM((SLOTS, pairs, rows, PAIR), bf16),
+            pltpu.VMEM((SLOTS, pairs, rows, 2 * PAIR), bf16),
+            pltpu.VMEM((SLOTS, rows, rows), f32),
+            pltpu.VMEM((pairs, rows, PAIR), f32),
             pltpu.VMEM((pairs, rows, PAIR), f32),
             pltpu.VMEM((pairs, rows, PAIR), f32),
             pltpu.VMEM((rows, width), bf16),

time: 50 us -> 42.7 us (0.85)
  Pallas kernels: 47.9 us -> 40.7 us
    pallas_call x1, Pallas kernels: 47.9 us -> 40.7 us  [body(): pl.pallas_call(functools.partial(kernel, n), out_shape=jax.ShapeDtypeStru...]
where the time goes in v2:
time: 42.7 us; the launch traced here: 42.6 us
  Pallas kernels  40.7 us (95%)
  local copies, waits for them, and re-layouts  1.87 us (4%)
    pallas_call x1, Pallas kernels, body(): pl.pallas_call(functools.partial(kernel, n), out_shape=jax.ShapeDtypeStru...  40.7 us
    unnamed x1, local copies, waits for them, and re-layouts  1.87 us

profile of v2, /device:TPU:0, one launch (start us, length us, event | category | flops | bytes accessed | tf_op | source)
XLA Modules:
  0.0 42.6 jit_solution(14682439856146071902)
XLA Ops:
  0.0 40.7 %shard_map.109 = bf16[512,512]{1,0:T(8,128)(2,1)} custom-call(bf16[512,512]{1,0:T(8,128)(2,1)} %atoms_hbm.1, s32[1,5,512,512]{3,2,1,0:T(8,128)} %mask_hbm.1, f32[1,512]{1,0:T(1,128)} %bitcast.3, bf16[512,512]{1,0:T(8,128)(2,1)} %wq_hbm.1, bf16[512,512]{1,0:T(8,128)(2,1)} %wk_hbm.1, bf16[512,512]{1,0:T(8,128)(2,1)} %wv_hbm.1, bf16[512,512]{1,0:T(8,128)(2,1)} %wo_hbm.1, ...), custom_call_target="tpu_custom_call" | custom-call | tf_op jit(solution)/shard_map/pallas_call | solution.py:346
  40.7 1.9 %copy.13 = bf16[512,512]{1,0:T(8,128)(2,1)} copy(bf16[512,512]{1,0:T(8,128)(2,1)} %shard_map.109) | data formatting | bytes 1048576
